TPU v7x, 32 devices: a whole 2x2x4 slice. The times are simulated.
32 devices in a mesh: row: 8 (over z, x), col: 4 (over y, core).
Axes of the slice: x: 2, y: 2, z: 4, core: 2. Of those that a mesh axis runs over, the one named last changes fastest.
Arguments:
- pair: bfloat16 [64, 64, 128], P('row', 'col'), may hold values from -6 to 6
- norm_in: float32 [128], replicated, may hold values from 0.1 to 1.9
- shift_in: float32 [128], replicated, may hold values from -3 to 3
- in_weight: bfloat16 [128, 640], replicated, may hold values from -0.5 to 0.5
- norm_out: float32 [128], replicated, may hold values from 0.1 to 1.9
- shift_out: float32 [128], replicated, may hold values from -3 to 3
- out_weight: bfloat16 [128, 128], replicated, may hold values from -0.5 to 0.5
Outputs:
- update: bfloat16 [64, 64, 128], P('row', 'col')
All inputs are finite; a program needn't handle non-finite values.
Results may differ from a plain program's by a relative error of at most 0.0054.
Values may be sent and summed in bfloat16 or wider, within the bound.
A program may use at most 64 MiB of HBM per device.

v0:
```python
import jax
import jax.numpy as jnp
from jax import lax
from jax.sharding import PartitionSpec as P

EPSILON = 1e-05


def layer_norm(values, gain, shift):
    values = values.astype(jnp.float32)
    center = jnp.mean(values, axis=-1, keepdims=True)
    spread = jnp.mean(jnp.square(values - center), axis=-1, keepdims=True)
    return (values - center) * lax.rsqrt(spread + EPSILON) * gain + shift


def local(pair, norm_in, shift_in, in_weight, norm_out, shift_out, out_weight):
    row_count, col_count, channels = pair.shape
    hidden = out_weight.shape[0]
    normed = layer_norm(pair, norm_in, shift_in).astype(jnp.bfloat16)
    projected = jnp.dot(normed.reshape(-1, channels), in_weight, preferred_element_type=jnp.float32)
    left = (jax.nn.sigmoid(projected[:, :hidden]) * projected[:, hidden : 2 * hidden]).astype(
        jnp.bfloat16
    )
    right = (
        jax.nn.sigmoid(projected[:, 2 * hidden : 3 * hidden])
        * projected[:, 3 * hidden : 4 * hidden]
    ).astype(jnp.bfloat16)
    gate = jax.nn.sigmoid(projected[:, 4 * hidden :]).reshape(row_count, col_count, channels)
    left = left.reshape(row_count, col_count, hidden)
    right = right.reshape(row_count, col_count, hidden)
    row_devices = lax.axis_size("row")
    col_devices = lax.axis_size("col")
    unit = row_count // col_devices
    groups = row_devices // col_devices
    sectioned = left.reshape(row_count, groups, col_devices, unit, hidden).transpose(0, 2, 1, 3, 4)
    sorted_parts = lax.all_to_all(sectioned, "col", split_axis=1, concat_axis=1, tiled=True)
    sorted_parts = sorted_parts.reshape(row_count, row_devices, unit * hidden)
    own_parts = lax.all_to_all(sorted_parts, "row", split_axis=1, concat_axis=0, tiled=True)
    own_parts = own_parts.reshape(row_count * row_devices, unit, hidden)
    right_full = lax.all_gather(right, "row", axis=0, tiled=True)
    mixed = jnp.einsum(
        "kih,kjh->ijh",
        lax.all_gather(own_parts, "col", axis=1, tiled=True),
        right_full,
        preferred_element_type=jnp.float32,
    )
    mixed_normed = layer_norm(mixed, norm_out, shift_out).astype(jnp.bfloat16)
    outward = jnp.dot(
        mixed_normed.reshape(-1, hidden), out_weight, preferred_element_type=jnp.float32
    )
    return (gate * outward.reshape(row_count, col_count, channels)).astype(jnp.bfloat16)


def solution(mesh):
    in_specs = (P("row", "col", None), P(), P(), P(), P(), P(), P())
    out_specs = P("row", "col", None)
    return jax.shard_map(local, mesh=mesh, in_specs=in_specs, out_specs=out_specs, check_vma=False)
```

profile of v0, /device:TPU:0, one launch (start us, length us, event | category | flops | bytes accessed | tf_op | source)
XLA Modules:
  0.0 71.7 jit_solution(3137486336146539258)
XLA Ops:
  0.0 0.0 copy-start
  0.0 0.9 %convert_reduce_fusion = f32[8,16]{1,0:T(8,128)S(1)} fusion(bf16[8,16,128]{2,1,0:T(8,128)(2,1)} %param.7), kind=kLoop, calls=%fused_computation.3 | loop fusion | flops 32640 | bytes 33280 | tf_op jit(solution)/shard_map/reduce_sum | solution.py:11
  0.9 0.9 %fusion.3 = f32[8,16]{1,0:T(8,128)S(1)} fusion(bf16[8,16,128]{2,1,0:T(8,128)(2,1)} %param.7, f32[8,16]{1,0:T(8,128)S(1)} %broadcast_multiply_fusion.1), kind=kLoop, calls=%fused_computation.6 | loop fusion | flops 65408 | bytes 33792 | tf_op jit(solution)/shard_map/reduce_sum | solution.py:12
  1.8 0.9 %fusion.6 = bf16[8,16,128]{2,1,0:T(8,128)(2,1)S(1)} fusion(bf16[8,16,128]{2,1,0:T(8,128)(2,1)} %param.7, f32[128]{0:T(128)} %param.9, f32[128]{0:T(128)} %param.8, f32[8,16]{1,0:T(8,128)S(1)} %add_rsqrt_fusion.1, f32[8,16]{1,0:T(8,128)S(1)} %broadcast_multiply_fusion.1), kind=kLoop, calls=%fused_computation.9 | loop fusion | flops 98304 | bytes 67584 | tf_op jit(solution)/shard_map/convert_element_type | solution.py:19
  2.7 0.2 fusion.23
  2.9 0.1 fusion.7
  3.0 0.6 copy.32
  3.6 4.3 %all-to-all-start = ((bf16[8,4,2,2,128]{4,3,2,0,1:T(2,128)(2,1)}), bf16[8,4,2,2,128]{4,3,2,0,1:T(2,128)(2,1)S(1)}, u32[]{:S(2)}, u32[]{:S(2)}) async-start(bf16[8,4,2,2,128]{4,3,2,0,1:T(2,128)(2,1)} %bitcast.30), calls=%async_computation | async-start | bytes 65536 | tf_op jit(solution)/shard_map/all_to_all | solution.py:36
  7.9 0.2 copy.22
  8.1 3.8 %all-to-all-done = bf16[8,4,2,2,128]{4,3,2,0,1:T(2,128)(2,1)S(1)} async-done(((bf16[8,4,2,2,128]{4,3,2,0,1:T(2,128)(2,1)}), bf16[8,4,2,2,128]{4,3,2,0,1:T(2,128)(2,1)S(1)}, u32[]{:S(2)}, u32[]{:S(2)}) %all-to-all-start) | async-done | bytes 32800 | tf_op jit(solution)/shard_map/all_to_all | solution.py:36
  11.9 0.6 reshape.54
  12.5 6.3 %all-to-all-start.1 = ((bf16[8,8,256]{2,0,1:T(8,128)(2,1)}), bf16[8,8,256]{2,0,1:T(8,128)(2,1)S(1)}, u32[]{:S(2)}, u32[]{:S(2)}) async-start(bf16[8,8,256]{2,0,1:T(8,128)(2,1)} %reshape.54), calls=%async_computation.1 | async-start | bytes 65536 | tf_op jit(solution)/shard_map/all_to_all | solution.py:38
  18.8 45.2 %all_gather.6 = bf16[64,16,128]{1,0,2:T(8,128)(2,1)S(1)} all-gather(bf16[8,16,128]{1,0,2:T(8,128)(2,1)S(1)} %copy.22), channel_id=1, replica_groups=mesh['row'=8,'col'=4] {'row'}, dimensions={0}, use_global_device_ids=true | all-gather | bytes 294912 | tf_op jit(solution)/shard_map/all_gather | solution.py:40
  64.0 0.0 all-to-all-done.1
  64.0 0.0 copy-start.1
  64.1 0.0 copy-start.2
  64.1 0.0 copy-start.3
  64.1 5.4 %all_gather.7 = bf16[64,8,128]{2,0,1:T(8,128)(2,1)S(1)} all-gather(bf16[64,2,128]{2,0,1:T(8,128)(2,1)S(1)} %copy.26), channel_id=1, replica_groups=mesh['row'=8,'col'=4] {'col'}, dimensions={1}, use_global_device_ids=true | all-gather | bytes 163840 | tf_op jit(solution)/shard_map/all_gather | solution.py:43
  69.5 0.2 copy.27
  69.7 0.7 fusion.24
  70.3 0.2 copy.28
  70.5 0.1 bitcast_reduce_fusion
  70.7 0.2 multiply_reduce_fusion
  70.9 0.8 %fusion = bf16[8,16,128]{2,1,0:T(8,128)(2,1)} fusion(f32[8,16,128]{2,1,0:T(8,128)S(1)} %bitcast.31, f32[128,16,8]{0,1,2:T(8,128)S(1)} %copy.28, bf16[128,128]{1,0:T(8,128)(2,1)S(1)} %copy-done.1, f32[128]{0:T(128)S(1)} %copy-done.2, f32[128]{0:T(128)S(1)} %copy-done.3, f32[8,16]{1,0:T(8,128)S(1)} %add_rsqrt_fusion, f32[8,16]{1,0:T(8,128)S(1)} %broadcast_multiply_fusion), kind=kOutput, calls=%fused_computation.1 | convolution fusion | flops 4308992 | bytes 198656 | tf_op jit(solution)/shard_map/dot_general | solution.py:48
  (11 shorter events, 0.1 us)
Async XLA Ops:
  0.0 2.7 %copy-start = (bf16[128,640]{1,0:T(8,128)(2,1)S(1)}, bf16[128,640]{1,0:T(8,128)(2,1)}, u32[]{:S(2)}) copy-start(bf16[128,640]{1,0:T(8,128)(2,1)} %param.10) | copy-start | bytes 491524
  3.6 8.2 %all-to-all-start = ((bf16[8,4,2,2,128]{4,3,2,0,1:T(2,128)(2,1)}), bf16[8,4,2,2,128]{4,3,2,0,1:T(2,128)(2,1)S(1)}, u32[]{:S(2)}, u32[]{:S(2)}) async-start(bf16[8,4,2,2,128]{4,3,2,0,1:T(2,128)(2,1)} %bitcast.30), calls=%async_computation | async-start | bytes 65536 | tf_op jit(solution)/shard_map/all_to_all | solution.py:36
  12.5 51.5 %all-to-all-start.1 = ((bf16[8,8,256]{2,0,1:T(8,128)(2,1)}), bf16[8,8,256]{2,0,1:T(8,128)(2,1)S(1)}, u32[]{:S(2)}, u32[]{:S(2)}) async-start(bf16[8,8,256]{2,0,1:T(8,128)(2,1)} %reshape.54), calls=%async_computation.1 | async-start | bytes 65536 | tf_op jit(solution)/shard_map/all_to_all | solution.py:38
  64.0 6.8 %copy-start.1 = (bf16[128,128]{1,0:T(8,128)(2,1)S(1)}, bf16[128,128]{1,0:T(8,128)(2,1)}, u32[]{:S(2)}) copy-start(bf16[128,128]{1,0:T(8,128)(2,1)} %param.13) | copy-start | bytes 98308
  64.1 6.8 %copy-start.2 = (f32[128]{0:T(128)S(1)}, f32[128]{0:T(128)}, u32[]{:S(2)}) copy-start(f32[128]{0:T(128)} %param.12) | copy-start | bytes 1540
  64.1 6.8 %copy-start.3 = (f32[128]{0:T(128)S(1)}, f32[128]{0:T(128)}, u32[]{:S(2)}) copy-start(f32[128]{0:T(128)} %param.11) | copy-start | bytes 1540
where the time goes:
time: 72.2 us; the launch traced here: 71.7 us
  blocking collectives  50.7 us (70%)
  starting transfers between devices  10.5 us (15%)
  waiting for transfers between devices  3.76 us (5%)
  other arithmetic  3.04 us (4%)
  local copies, waits for them, and re-layouts  1.92 us (3%)
  matrix products  1.67 us (2%)
    all_gather x1, blocking collectives, local(): right_full = lax.all_gather(right, 'row', axis=0, tiled=True)  45.2 us
    all_to_all x1, starting transfers between devices, local(): lax.all_to_all(sorted_parts, 'row', split_axis=1, concat_axis=0, tiled=True)  6.25 us
    all_gather x1, blocking collectives, local(): lax.all_gather(own_parts, 'col', axis=1, tiled=True)  5.42 us
    all_to_all x1, starting transfers between devices, local(): lax.all_to_all(sectioned, 'col', split_axis=1, concat_axis=1, tiled=True)  4.26 us
    all_to_all x1, waiting for transfers between devices, local(): lax.all_to_all(sectioned, 'col', split_axis=1, concat_axis=1, tiled=True)  3.76 us
  transfers between devices with their start and end apart: 2, of which 1 were waited for; matrix products, arithmetic and copies ran while one was open for 0% of the time, Pallas kernels for 0%

commit v1 on v0

--- a/solution.py
+++ b/solution.py
@@ -4,6 +4,21 @@
 from jax.sharding import PartitionSpec as P
 
 EPSILON = 1e-05
+
+
+def work_around(x, axis, dim, make, out_dim):
+    ways, here, step = (lax.axis_size(axis), lax.axis_index(axis), x.shape[dim])
+    results = []
+    for far in range(ways):
+        arriving = (
+            lax.ppermute(x, axis, [(d, (d + 1) % ways) for d in range(ways)])
+            if far + 1 < ways
+            else x
+        )
+        results.append(make(x, (here - far) % ways * step))
+        x = arriving
+    line = jnp.concatenate(results[::-1], axis=out_dim)
+    return jnp.roll(line, (here + 1) * results[0].shape[out_dim], axis=out_dim)
 
 
 def layer_norm(values, gain, shift):
@@ -38,11 +53,14 @@
     own_parts = lax.all_to_all(sorted_parts, "row", split_axis=1, concat_axis=0, tiled=True)
     own_parts = own_parts.reshape(row_count * row_devices, unit, hidden)
     right_full = lax.all_gather(right, "row", axis=0, tiled=True)
-    mixed = jnp.einsum(
-        "kih,kjh->ijh",
-        lax.all_gather(own_parts, "col", axis=1, tiled=True),
-        right_full,
-        preferred_element_type=jnp.float32,
+    mixed = work_around(
+        own_parts,
+        "col",
+        1,
+        lambda own_block, offset: jnp.einsum(
+            "kih,kjh->ijh", own_block, right_full, preferred_element_type=jnp.float32
+        ),
+        0,
     )
     mixed_normed = layer_norm(mixed, norm_out, shift_out).astype(jnp.bfloat16)
     outward = jnp.dot(

time: 72.2 us -> 77.7 us (1.076)
  waiting for transfers between devices: 3.76 us -> 12.7 us
  blocking collectives: 50.7 us -> 45.2 us
  matrix products: 1.67 us -> 3.62 us
    ppermute x0 -> x3, waiting for transfers between devices: none -> 8.91 us  [work_around(): lax.ppermute(x, axis, [(d, (d + 1) % ways) for d in range(ways)])]
    all_gather x1 -> x0, blocking collectives: 5.42 us -> none  [local(): lax.all_gather(own_parts, 'col', axis=1, tiled=True)]
    dot_general x1 -> x4, matrix products: 0.65 us -> 2.6 us  [local(): jnp.einsum('kih,kjh->ijh', own_block, right_full, preferred_element_type=...]
  transfers between devices with their start and end apart: 2 -> 5, of which waited for: 1 -> 4; matrix products, arithmetic and copies ran while one was open for 0% -> 3% of each run, Pallas kernels for 0% -> 0%
where the time goes in v1:
time: 77.7 us; the launch traced here: 77.3 us
  blocking collectives  45.2 us (58%)
  waiting for transfers between devices  12.7 us (16%)
  starting transfers between devices  10.6 us (14%)
  matrix products  3.62 us (5%)
  other arithmetic  3.02 us (4%)
  local copies, waits for them, and re-layouts  1.93 us (2%)
    all_gather x1, blocking collectives, local(): right_full = lax.all_gather(right, 'row', axis=0, tiled=True)  45.2 us
    ppermute x3, waiting for transfers between devices, work_around(): lax.ppermute(x, axis, [(d, (d + 1) % ways) for d in range(ways)])  8.91 us
    all_to_all x1, starting transfers between devices, local(): lax.all_to_all(sorted_parts, 'row', split_axis=1, concat_axis=0, tiled=True)  6.25 us
    all_to_all x1, starting transfers between devices, local(): lax.all_to_all(sectioned, 'col', split_axis=1, concat_axis=1, tiled=True)  4.26 us
    all_to_all x1, waiting for transfers between devices, local(): lax.all_to_all(sectioned, 'col', split_axis=1, concat_axis=1, tiled=True)  3.76 us
    dot_general x4, matrix products, local(): jnp.einsum('kih,kjh->ijh', own_block, right_full, preferred_element_type=...  2.6 us
  transfers between devices with their start and end apart: 5, of which 4 were waited for; matrix products, arithmetic and copies ran while one was open for 3% of the time, Pallas kernels for 0%

profile of v1, /device:TPU:0, one launch (start us, length us, event | category | flops | bytes accessed | tf_op | source)
XLA Modules:
  0.0 77.3 jit_solution(12437827089898417168)
XLA Ops:
  0.0 0.9 %convert_reduce_fusion = f32[8,16]{1,0:T(8,128)S(1)} fusion(bf16[8,16,128]{2,1,0:T(8,128)(2,1)} %param.7), kind=kLoop, calls=%fused_computation.7 | loop fusion | flops 32640 | bytes 33280 | tf_op jit(solution)/shard_map/reduce_sum | solution.py:26
  0.9 0.9 %fusion.3 = f32[8,16]{1,0:T(8,128)S(1)} fusion(bf16[8,16,128]{2,1,0:T(8,128)(2,1)} %param.7, f32[8,16]{1,0:T(8,128)S(1)} %broadcast_multiply_fusion.1), kind=kLoop, calls=%fused_computation.10 | loop fusion | flops 65408 | bytes 33792 | tf_op jit(solution)/shard_map/reduce_sum | solution.py:27
  1.8 0.9 %fusion.6 = bf16[8,16,128]{2,1,0:T(8,128)(2,1)S(1)} fusion(bf16[8,16,128]{2,1,0:T(8,128)(2,1)} %param.7, f32[128]{0:T(128)} %param.9, f32[128]{0:T(128)} %param.8, f32[8,16]{1,0:T(8,128)S(1)} %add_rsqrt_fusion.1, f32[8,16]{1,0:T(8,128)S(1)} %broadcast_multiply_fusion.1), kind=kLoop, calls=%fused_computation.13 | loop fusion | flops 98304 | bytes 67584 | tf_op jit(solution)/shard_map/convert_element_type | solution.py:34
  2.7 0.2 fusion.24
  2.9 0.1 fusion.7
  3.0 0.6 copy.33
  3.6 4.3 %all-to-all-start = ((bf16[8,4,2,2,128]{4,3,2,0,1:T(2,128)(2,1)}), bf16[8,4,2,2,128]{4,3,2,0,1:T(2,128)(2,1)S(1)}, u32[]{:S(2)}, u32[]{:S(2)}) async-start(bf16[8,4,2,2,128]{4,3,2,0,1:T(2,128)(2,1)} %bitcast.36), calls=%async_computation | async-start | bytes 65536 | tf_op jit(solution)/shard_map/all_to_all | solution.py:51
  7.9 0.2 copy.16
  8.1 3.8 %all-to-all-done = bf16[8,4,2,2,128]{4,3,2,0,1:T(2,128)(2,1)S(1)} async-done(((bf16[8,4,2,2,128]{4,3,2,0,1:T(2,128)(2,1)}), bf16[8,4,2,2,128]{4,3,2,0,1:T(2,128)(2,1)S(1)}, u32[]{:S(2)}, u32[]{:S(2)}) %all-to-all-start) | async-done | bytes 32800 | tf_op jit(solution)/shard_map/all_to_all | solution.py:51
  11.9 0.6 reshape.54
  12.5 6.3 %all-to-all-start.1 = ((bf16[8,8,256]{2,0,1:T(8,128)(2,1)}), bf16[8,8,256]{2,0,1:T(8,128)(2,1)S(1)}, u32[]{:S(2)}, u32[]{:S(2)}) async-start(bf16[8,8,256]{2,0,1:T(8,128)(2,1)} %reshape.54), calls=%async_computation.1 | async-start | bytes 65536 | tf_op jit(solution)/shard_map/all_to_all | solution.py:53
  18.8 45.2 %all_gather.3 = bf16[64,16,128]{1,0,2:T(8,128)(2,1)S(1)} all-gather(bf16[8,16,128]{1,0,2:T(8,128)(2,1)S(1)} %copy.16), channel_id=1, replica_groups=mesh['row'=8,'col'=4] {'row'}, dimensions={0}, use_global_device_ids=true | all-gather | bytes 294912 | tf_op jit(solution)/shard_map/all_gather | solution.py:55
  64.0 0.1 copy.20
  64.2 0.7 convolution_bitcast_fusion
  64.9 0.1 copy.25
  64.9 3.0 %collective-permute-done = bf16[64,2,128]{0,1,2:T(2,128)(2,1)S(1)} collective-permute-done((bf16[64,2,128]{0,1,2:T(2,128)(2,1)S(1)}, bf16[64,2,128]{0,1,2:T(2,128)(2,1)S(1)}, u32[]{:S(2)}, u32[]{:S(2)}) %collective-permute-start) | collective-permute-done | bytes 32800 | tf_op jit(solution)/shard_map/ppermute | solution.py:14
  67.9 0.7 convolution_bitcast_fusion.1
  68.6 3.0 %collective-permute-done.1 = bf16[64,2,128]{0,1,2:T(2,128)(2,1)S(1)} collective-permute-done((bf16[64,2,128]{0,1,2:T(2,128)(2,1)S(1)}, bf16[64,2,128]{0,1,2:T(2,128)(2,1)S(1)}, u32[]{:S(2)}, u32[]{:S(2)}) %collective-permute-start.1) | collective-permute-done | bytes 32800 | tf_op jit(solution)/shard_map/ppermute | solution.py:14
  71.6 0.7 convolution_bitcast_fusion.2
  72.3 3.0 %collective-permute-done.2 = bf16[64,2,128]{0,1,2:T(2,128)(2,1)S(1)} collective-permute-done((bf16[64,2,128]{0,1,2:T(2,128)(2,1)S(1)}, bf16[64,2,128]{0,1,2:T(2,128)(2,1)S(1)}, u32[]{:S(2)}, u32[]{:S(2)}) %collective-permute-start.2) | collective-permute-done | bytes 32800 | tf_op jit(solution)/shard_map/ppermute | solution.py:14
  75.3 0.6 convolution_bitcast_fusion.3
  76.1 0.1 dynamic-slice_reduce_fusion
  76.2 0.2 multiply_reduce_fusion
  76.4 0.8 %fusion = bf16[8,16,128]{2,1,0:T(8,128)(2,1)} fusion(f32[8,16,128]{2,1,0:T(8,128)S(1)} %bitcast.37, f32[16,16,128]{2,1,0:T(8,128)S(1)} %constant_dynamic-update-slice_fusion, s32[]{:T(128)S(6)} %select_n.14, bf16[128,128]{1,0:T(8,128)(2,1)S(1)} %copy-done.1, f32[128]{0:T(128)S(1)} %copy-done.2, f32[128]{0:T(128)S(1)} %copy-done.3, ...), kind=kOutput, calls=%fused_computation.5 | convolution fusion | flops 4308992 | bytes 205828 | tf_op jit(solution)/shard_map/dot_general | solution.py:66
  (29 shorter events, 0.4 us)
Async XLA Ops:
  0.0 2.7 %copy-start = (bf16[128,640]{1,0:T(8,128)(2,1)S(1)}, bf16[128,640]{1,0:T(8,128)(2,1)}, u32[]{:S(2)}) copy-start(bf16[128,640]{1,0:T(8,128)(2,1)} %param.10) | copy-start | bytes 491524
  3.6 8.2 %all-to-all-start = ((bf16[8,4,2,2,128]{4,3,2,0,1:T(2,128)(2,1)}), bf16[8,4,2,2,128]{4,3,2,0,1:T(2,128)(2,1)S(1)}, u32[]{:S(2)}, u32[]{:S(2)}) async-start(bf16[8,4,2,2,128]{4,3,2,0,1:T(2,128)(2,1)} %bitcast.36), calls=%async_computation | async-start | bytes 65536 | tf_op jit(solution)/shard_map/all_to_all | solution.py:51
  12.5 51.5 %all-to-all-start.1 = ((bf16[8,8,256]{2,0,1:T(8,128)(2,1)}), bf16[8,8,256]{2,0,1:T(8,128)(2,1)S(1)}, u32[]{:S(2)}, u32[]{:S(2)}) async-start(bf16[8,8,256]{2,0,1:T(8,128)(2,1)} %reshape.54), calls=%async_computation.1 | async-start | bytes 65536 | tf_op jit(solution)/shard_map/all_to_all | solution.py:53
  64.2 3.7 %collective-permute-start = (bf16[64,2,128]{0,1,2:T(2,128)(2,1)S(1)}, bf16[64,2,128]{0,1,2:T(2,128)(2,1)S(1)}, u32[]{:S(2)}, u32[]{:S(2)}) collective-permute-start(bf16[64,2,128]{0,1,2:T(2,128)(2,1)S(1)} %copy.20), channel_id=1, source_target_pairs={{0,1},{1,2},{2,3},{3,0},{4,5},{5,6},{6,7},{7,4},{8,9},{9,10},{10,1... | collective-permute-start | bytes 98312 | tf_op jit(solution)/shard_map/ppermute | solution.py:14
  67.9 3.7 %collective-permute-start.1 = (bf16[64,2,128]{0,1,2:T(2,128)(2,1)S(1)}, bf16[64,2,128]{0,1,2:T(2,128)(2,1)S(1)}, u32[]{:S(2)}, u32[]{:S(2)}) collective-permute-start(bf16[64,2,128]{0,1,2:T(2,128)(2,1)S(1)} %collective-permute-done), channel_id=1, source_target_pairs={{0,1},{1,2},{2,3},{3,0},{4,5},{5,6},{6,7},{7,4},{8,9},{9,10},{10,1... | collective-permute-start | bytes 98312 | tf_op jit(solution)/shard_map/ppermute | solution.py:14
  68.6 7.8 %copy-start.1 = (bf16[128,128]{1,0:T(8,128)(2,1)S(1)}, bf16[128,128]{1,0:T(8,128)(2,1)}, u32[]{:S(2)}) copy-start(bf16[128,128]{1,0:T(8,128)(2,1)} %param.13) | copy-start | bytes 98308
  68.6 7.8 %copy-start.2 = (f32[128]{0:T(128)S(1)}, f32[128]{0:T(128)}, u32[]{:S(2)}) copy-start(f32[128]{0:T(128)} %param.12) | copy-start | bytes 1540
  68.6 7.8 %copy-start.3 = (f32[128]{0:T(128)S(1)}, f32[128]{0:T(128)}, u32[]{:S(2)}) copy-start(f32[128]{0:T(128)} %param.11) | copy-start | bytes 1540
  71.6 3.7 %collective-permute-start.2 = (bf16[64,2,128]{0,1,2:T(2,128)(2,1)S(1)}, bf16[64,2,128]{0,1,2:T(2,128)(2,1)S(1)}, u32[]{:S(2)}, u32[]{:S(2)}) collective-permute-start(bf16[64,2,128]{0,1,2:T(2,128)(2,1)S(1)} %collective-permute-done.1), channel_id=1, source_target_pairs={{0,1},{1,2},{2,3},{3,0},{4,5},{5,6},{6,7},{7,4},{8,9},{9,10},{10,1... | collective-permute-start | bytes 98312 | tf_op jit(solution)/shard_map/ppermute | solution.py:14
